TPU v7x, 32 devices: a whole 2x2x4 slice. The times are simulated.
32 devices in a mesh: ctx: 16 (over z, y, core), head: 2 (over x).
Axes of the slice: x: 2, y: 2, z: 4, core: 2. Of those that a mesh axis runs over, the one named last changes fastest.
Arguments:
- queries: bfloat16 [2048, 2048], P('ctx', 'head'), may hold values from -100 to 100
- keys: bfloat16 [2048, 2048], P('ctx', 'head'), may hold values from -50 to 50
- values: bfloat16 [2048, 2048], P('ctx', 'head'), may hold values from -6 to 6
- out_weight: bfloat16 [2048, 4096], P('head'), may hold values from -0.125 to 0.125
- mixed_grad: bfloat16 [2048, 4096], P('ctx', 'head'), may hold values from -6 to 6
- lengths: int32 [16], replicated, may hold values from 1 to 384, 2048 in all
- dilation: int32 [16], P('head'), may hold values from 1 to 8
Outputs:
- mixed: bfloat16 [2048, 4096], P('ctx', 'head')
- grad_queries: bfloat16 [2048, 2048], P('ctx', 'head')
- grad_keys: bfloat16 [2048, 2048], P('ctx', 'head')
- grad_values: bfloat16 [2048, 2048], P('ctx', 'head')
Inputs may be any that keep to these rules, and one draw needn't show every extreme that they name: The lengths sum to 2048, and the longest document has exactly 384 tokens.
All inputs are finite; a program needn't handle non-finite values.
Results may differ from a plain program's by a relative error of at most 0.029.
Values may be sent and summed in bfloat16 or wider, within the bound.
A program may use at most 64 MiB of HBM per device.

v0:
```python
import functools
import jax
import jax.numpy as jnp
from jax import lax
from jax.experimental import pallas as pl
from jax.experimental.pallas import tpu as pltpu
from jax.sharding import PartitionSpec as P

HALF = 32
MAXD = 8
FAR = 1e6
NEG = -1e30


def attend_kernel(
    row_count, total, factor, first, index_ref, bound_ref, inv_ref,
    q_ref, go_ref, own_ref, a_ref, b_ref, po_ref, pa_ref,
    att_ref, gq_ref, own_t, a_t, b_t, po_t, pa_t, dist,
):
    slabs = (own_ref, a_ref, b_ref, po_ref, pa_ref)
    outs = (own_t, a_t, b_t, po_t, pa_t)

    @pl.when(pl.program_id(0) == 0)
    def _():
        me = index_ref[0]
        sign = 1 - 2 * lax.rem(me, 2)
        ndocs = bound_ref.shape[0]

        def segment(pos):
            seg = jnp.zeros(pos.shape, jnp.int32)
            for n in range(ndocs):
                seg = seg + (pos >= bound_ref[n]).astype(jnp.int32)
            return seg

        qpos = me * row_count + lax.broadcasted_iota(jnp.int32, (1, row_count), 1)
        qseg = segment(qpos)
        for i, off in enumerate((0, 2, -2, 1, -1)):
            kpos = (me + sign * off) * row_count + lax.broadcasted_iota(
                jnp.int32, (row_count, row_count), 0
            )
            same = (segment(kpos) == qseg) & (kpos >= 0) & (kpos < total)
            gap = jnp.abs(kpos - qpos).astype(jnp.float32)
            dist[pl.ds(i * row_count, row_count), :] = jnp.where(same, gap, FAR)

    inv = inv_ref[first + pl.program_id(0)]
    steps = dist[...] * inv
    whole = jnp.floor(steps + 0.5)
    mask = (whole <= HALF) & (jnp.abs(steps - whole) < 0.01)
    q = q_ref[...]
    go = go_ref[...]
    k = jnp.concatenate([r[0] for r in slabs], axis=0)
    v = jnp.concatenate([r[1] for r in slabs], axis=0)
    nt = (((1,), (1,)), ((), ()))
    tn = (((0,), (0,)), ((), ()))
    f32 = jnp.float32
    scores = lax.dot_general(k, q, nt, preferred_element_type=f32) * factor
    scores = jnp.where(mask, scores, NEG)
    top = jnp.max(scores, axis=0, keepdims=True)
    e = jnp.exp(scores - top)
    w = e * (1.0 / jnp.sum(e, axis=0, keepdims=True))
    p = w.astype(jnp.bfloat16)
    gp = lax.dot_general(v, go, nt, preferred_element_type=f32)
    delta = jnp.sum(w * gp, axis=0, keepdims=True)
    s = (w * (gp - delta)).astype(jnp.bfloat16)
    att_ref[...] = lax.dot_general(p, v, tn, preferred_element_type=f32).astype(jnp.bfloat16)
    gq_ref[...] = (
        lax.dot_general(s, k, tn, preferred_element_type=f32) * factor
    ).astype(jnp.bfloat16)
    kt = (jnp.dot(s, q, preferred_element_type=f32) * factor).astype(jnp.bfloat16)
    vt = jnp.dot(p, go, preferred_element_type=f32).astype(jnp.bfloat16)
    for i, out in enumerate(outs):
        out[0] = kt[i * row_count : (i + 1) * row_count]
        out[1] = vt[i * row_count : (i + 1) * row_count]


def attend(index, bounds, inv, q, go, slabs, first, total, factor, width):
    rows, cols = q.shape[0], slabs[0].shape[2]
    heads = cols // width
    smem = pl.BlockSpec(memory_space=pltpu.SMEM)
    shared = pl.BlockSpec((rows, width), lambda h: (0, first + h))
    flat = pl.BlockSpec((rows, width), lambda h: (0, h))
    pair = pl.BlockSpec((2, rows, width), lambda h: (0, 0, h))
    one = jax.ShapeDtypeStruct((rows, cols), jnp.bfloat16)
    two = jax.ShapeDtypeStruct((2, rows, cols), jnp.bfloat16)
    return pl.pallas_call(
        functools.partial(attend_kernel, rows, total, factor, first),
        grid=(heads,),
        in_specs=[smem, smem, smem, shared, shared] + [pair] * 5,
        out_specs=[flat, flat] + [pair] * 5,
        out_shape=[one, one] + [two] * 5,
        scratch_shapes=[pltpu.VMEM((5 * rows, rows), jnp.float32)],
        compiler_params=pltpu.CompilerParams(dimension_semantics=("arbitrary",)),
        cost_estimate=pl.CostEstimate(
            flops=heads * 6 * 2 * 5 * rows * rows * width * 8,
            bytes_accessed=24 * 2 * rows * cols,
            transcendentals=heads * 5 * rows * rows,
        ),
    )(index, bounds, inv, q, go, *slabs)


def per_device(queries, keys, values, out_weight, mixed_grad, lengths, dilation):
    rows = queries.shape[0]
    local_heads = dilation.shape[0]
    width = queries.shape[1] // local_heads
    factor = width ** (-0.5)
    count = lax.axis_size("ctx")
    sides = lax.axis_size("head")
    total = rows * count
    assert 2 * rows >= HALF * MAXD and count % 2 == 0
    index = lax.axis_index("ctx").astype(jnp.int32).reshape(1)
    bounds = jnp.cumsum(lengths).astype(jnp.int32)
    inv = 1.0 / dilation.astype(jnp.float32)

    inward = [
        (j, t) for j in range(count) for t in [j - 2 if j % 2 == 0 else j + 2] if 0 <= t < count
    ]
    outward = [(t, j) for j, t in inward]
    swapped = [(j, j ^ 1) for j in range(count)]

    def move(x, pairs):
        return lax.ppermute(x, "ctx", pairs)

    groups = 2 if local_heads % 2 == 0 else 1
    gh = local_heads // groups
    cut = [slice(g * gh * width, (g + 1) * gh * width) for g in range(groups)]
    half = mixed_grad.shape[1]
    if sides == 2:
        other = lax.ppermute(mixed_grad, "head", [(0, 1), (1, 0)])
        left = lax.axis_index("head") == 0
        grad_full = jnp.concatenate(
            [jnp.where(left, mixed_grad, other), jnp.where(left, other, mixed_grad)], axis=1
        )
    else:
        grad_full = lax.all_gather(mixed_grad, "head", axis=1, tiled=True)
    stacks = []
    for g in range(groups):
        own = jnp.stack([keys[:, cut[g]], values[:, cut[g]]])
        a = move(own, inward)
        stacks.append((own, a, move(own, outward), move(own, swapped), move(a, swapped)))
    grad_attention = lax.dot_general(
        grad_full, out_weight, (((1,), (1,)), ((), ())), preferred_element_type=jnp.float32
    ).astype(jnp.bfloat16)

    atts, gqs, gkvs = [], [], []
    f32 = jnp.float32
    for g in range(groups):
        att, gq, own_t, a_t, b_t, po_t, pa_t = attend(
            index, bounds, inv, queries, grad_attention, stacks[g], g * gh, total, factor, width
        )
        pa_back = move(pa_t, swapped)
        b_back = move(b_t, inward)
        po_back = move(po_t, swapped)
        a_sum = (a_t.astype(f32) + pa_back.astype(f32)).astype(jnp.bfloat16)
        a_back = move(a_sum, outward)
        gkvs.append(
            (
                own_t.astype(f32) + po_back.astype(f32) + b_back.astype(f32) + a_back.astype(f32)
            ).astype(jnp.bfloat16)
        )
        atts.append(att)
        gqs.append(gq)
    attention = jnp.concatenate(atts, axis=1)
    partial = jnp.dot(attention, out_weight, preferred_element_type=f32)
    if sides == 2:
        lo, hi = partial[:, :half], partial[:, half:]
        away = jnp.where(left, hi, lo).astype(jnp.bfloat16)
        came = lax.ppermute(away, "head", [(0, 1), (1, 0)])
        mixed = (jnp.where(left, lo, hi) + came.astype(f32)).astype(jnp.bfloat16)
    else:
        mixed = lax.psum_scatter(
            partial.astype(jnp.bfloat16), "head", scatter_dimension=1, tiled=True
        )
    gkv = jnp.concatenate(gkvs, axis=2)
    return mixed, jnp.concatenate(gqs, axis=1), gkv[0], gkv[1]


def solution(mesh):
    both = P("ctx", "head")
    return jax.shard_map(
        per_device,
        mesh=mesh,
        in_specs=(both, both, both, P("head", None), both, P(), P("head")),
        out_specs=(both, both, both, both),
        check_vma=False,
    )
```

profile of v0, /device:TPU:9, one launch (start us, length us, event | category | flops | bytes accessed | tf_op | source)
XLA Modules:
  0.0 83.0 jit_solution(12156209052276287371)
XLA Ops:
  0.6 1.3 %collective-permute-start = (bf16[128,2048]{1,0:T(8,128)(2,1)}, bf16[128,2048]{1,0:T(8,128)(2,1)S(1)}, u32[]{:S(2)}, u32[]{:S(2)}) collective-permute-start(bf16[128,2048]{1,0:T(8,128)(2,1)} %param.11), channel_id=1, source_target_pairs={{0,1},{1,0},{2,3},{3,2},{4,5},{5,4},{6,7},{7,6},{8,9},{9,8},{10,11... | collective-permute-start | bytes 1572872 | tf_op jit(solution)/shard_map/ppermute | solution.py:128
  1.9 1.1 %slice_bitcast_fusion.2 = (bf16[1,128,512]{2,1,0:T(8,128)(2,1)S(1)}, bf16[1,128,512]{2,1,0:T(8,128)(2,1)S(1)}, bf16[1,128,512]{2,1,0:T(8,128)(2,1)S(1)}, bf16[1,128,512]{2,1,0:T(8,128)(2,1)S(1)}) fusion(bf16[128,1024]{1,0:T(8,128)(2,1)} %param.9, bf16[128,1024]{1,0:T(8,128)(2,1)} %param.8), kind=kLoop, calls=%fused_computation.27 | loop fusion | bytes 1048576 | tf_op jit(solution)/shard_map/stack | solution.py:137
  3.1 0.0 copy-start.5
  3.1 3.1 %collective-permute-start.1 = (bf16[2,128,512]{2,1,0:T(8,128)(2,1)S(1)}, bf16[2,128,512]{2,1,0:T(8,128)(2,1)S(1)}, u32[]{:S(2)}, u32[]{:S(2)}) collective-permute-start(bf16[2,128,512]{2,1,0:T(8,128)(2,1)S(1)} %pad_maximum_fusion.1.own_ref), channel_id=1, source_target_pairs={{2,6},{4,0},{6,10},{8,4},{10,14},{12,8},{14,18},{16,12},{18,22},{2... | collective-permute-start | bytes 786440 | tf_op jit(solution)/shard_map/ppermute | solution.py:121
  6.2 3.0 %collective-permute-start.2 = (bf16[2,128,512]{2,1,0:T(8,128)(2,1)S(1)}, bf16[2,128,512]{2,1,0:T(8,128)(2,1)S(1)}, u32[]{:S(2)}, u32[]{:S(2)}) collective-permute-start(bf16[2,128,512]{2,1,0:T(8,128)(2,1)S(1)} %pad_maximum_fusion.1.own_ref), channel_id=1, source_target_pairs={{6,2},{0,4},{10,6},{4,8},{14,10},{8,12},{18,14},{12,16},{22,18},{1... | collective-permute-start | bytes 786440 | tf_op jit(solution)/shard_map/ppermute | solution.py:121
  9.3 0.7 collective-permute-start.3
  10.0 0.0 copy-start.4
  10.0 4.0 %collective-permute-start.5 = (bf16[2,128,512]{2,1,0:T(8,128)(2,1)S(1)}, bf16[2,128,512]{2,1,0:T(8,128)(2,1)S(1)}, u32[]{:S(2)}, u32[]{:S(2)}) collective-permute-start(bf16[2,128,512]{2,1,0:T(8,128)(2,1)S(1)} %pad_maximum_fusion.2.own_ref), channel_id=1, source_target_pairs={{2,6},{4,0},{6,10},{8,4},{10,14},{12,8},{14,18},{16,12},{18,22},{2... | collective-permute-start | bytes 786440 | tf_op jit(solution)/shard_map/ppermute | solution.py:121
  14.1 0.7 copy.12
  14.8 0.7 reduce.bound_ref
  15.5 1.2 %convert_divide_fusion.inv_ref = f32[8]{0:T(128)} fusion(s32[8]{0:T(128)} %param.13), kind=kLoop, calls=%fused_computation.29 | loop fusion | flops 16 | bytes 64 | tf_op jit(solution)/shard_map/div | solution.py:112
  16.7 0.0 collective-permute-done.1.a_ref
  16.7 2.8 %collective-permute-start.6 = (bf16[2,128,512]{2,1,0:T(8,128)(2,1)S(1)}, bf16[2,128,512]{2,1,0:T(8,128)(2,1)S(1)}, u32[]{:S(2)}, u32[]{:S(2)}) collective-permute-start(bf16[2,128,512]{2,1,0:T(8,128)(2,1)S(1)} %pad_maximum_fusion.2.own_ref), channel_id=1, source_target_pairs={{6,2},{0,4},{10,6},{4,8},{14,10},{8,12},{18,14},{12,16},{22,18},{1... | collective-permute-start | bytes 786440 | tf_op jit(solution)/shard_map/ppermute | solution.py:121
  19.5 0.0 collective-permute-done
  19.6 5.4 %collective-permute-start.4 = (bf16[2,128,512]{2,1,0:T(8,128)(2,1)S(1)}, bf16[2,128,512]{2,1,0:T(8,128)(2,1)S(1)}, u32[]{:S(2)}, u32[]{:S(2)}) collective-permute-start(bf16[2,128,512]{2,1,0:T(8,128)(2,1)S(1)} %collective-permute-done.1.a_ref), channel_id=1, source_target_pairs={{0,2},{2,0},{4,6},{6,4},{8,10},{10,8},{12,14},{14,12},{16,18},{18,... | collective-permute-start | bytes 786440 | tf_op jit(solution)/shard_map/ppermute | solution.py:121
  24.9 1.1 %broadcast_select_fusion.1 = (bf16[128,2048]{1,0:T(8,128)(2,1)S(1)}, bf16[128,2048]{1,0:T(8,128)(2,1)S(1)}) fusion(bf16[128,2048]{1,0:T(8,128)(2,1)} %param.11, bf16[128,2048]{1,0:T(8,128)(2,1)S(1)} %collective-permute-done, pred[]{:T(512)S(6)} %eq.3), kind=kLoop, calls=%fused_computation.13 | loop fusion | flops 524288 | bytes 2097153 | tf_op jit(solution)/shard_map/jit(_where)/select_n | solution.py:131
  26.0 7.0 %convolution_convert_fusion.go_ref = bf16[128,1024]{1,0:T(8,128)(2,1)} fusion(bf16[1024,4096]{1,0:T(8,128)(2,1)} %param.10, bf16[128,2048]{1,0:T(8,128)(2,1)S(1)} %get-tuple-element.33, bf16[128,2048]{1,0:T(8,128)(2,1)S(1)} %get-tuple-element.32), kind=kOutput, calls=%fused_computation | convolution fusion | flops 1075970048 | bytes 9699328 | tf_op jit(solution)/shard_map/dot_general | solution.py:140
  33.0 0.0 collective-permute-done.2.b_ref
  33.0 0.0 collective-permute-start.7
  33.0 0.0 collective-permute-done.5.a_ref
  33.0 0.5 collective-permute-start.8
  33.6 0.2 copy-done.11
  33.7 0.5 copy-done.12
  34.2 0.1 copy-done.17
  34.3 6.1 %shard_map.102 = (bf16[128,512]{1,0:T(8,128)(2,1)}, bf16[128,512]{1,0:T(8,128)(2,1)}, bf16[2,128,512]{2,1,0:T(8,128)(2,1)}, bf16[2,128,512]{2,1,0:T(8,128)(2,1)}...) custom-call(s32[1]{0:T(128)} %bitcast.index_ref, s32[16]{0:T(128)} %reduce.bound_ref, ...), custom_call_target="tpu_custom_call" | custom-call | flops 4026531840 | bytes 3145728 | tf_op jit(solution)/shard_map/pallas_call | solution.py:85
  40.5 0.2 collective-permute-start.12
  40.6 0.4 collective-permute-start.10
  41.0 4.6 %collective-permute-start.11 = (bf16[2,128,512]{2,1,0:T(8,128)(2,1)}, bf16[2,128,512]{2,1,0:T(8,128)(2,1)S(1)}, u32[]{:S(2)}, u32[]{:S(2)}) collective-permute-start(bf16[2,128,512]{2,1,0:T(8,128)(2,1)} %get-tuple-element.24), channel_id=1, source_target_pairs={{2,6},{4,0},{6,10},{8,4},{10,14},{12,8},{14,18},{16,12},{18,22},{2... | collective-permute-start | bytes 786440 | tf_op jit(solution)/shard_map/ppermute | solution.py:121
  45.7 0.7 copy-done.15
  46.4 0.7 copy-done.16
  47.1 6.2 %shard_map.103 = (bf16[128,512]{1,0:T(8,128)(2,1)}, bf16[128,512]{1,0:T(8,128)(2,1)}, bf16[2,128,512]{2,1,0:T(8,128)(2,1)}, bf16[2,128,512]{2,1,0:T(8,128)(2,1)}...) custom-call(s32[1]{0:T(128)} %bitcast.index_ref, s32[16]{0:T(128)} %reduce.bound_ref, ...), custom_call_target="tpu_custom_call" | custom-call | flops 4026531840 | bytes 3145728 | tf_op jit(solution)/shard_map/pallas_call | solution.py:85
  53.3 0.3 collective-permute-start.16
  53.6 0.2 collective-permute-start.14
  53.9 4.8 %fusion.6 = f32[128,4096]{1,0:T(8,128)S(1)} fusion(bf16[1024,4096]{1,0:T(8,128)(2,1)} %param.10, bf16[128,512]{1,0:T(8,128)(2,1)} %get-tuple-element.19, bf16[128,512]{1,0:T(8,128)(2,1)S(1)} %copy-done.6), kind=kOutput, calls=%fused_computation.20 | convolution fusion | flops 1074266112 | bytes 10747904 | tf_op jit(solution)/shard_map/dot_general | solution.py:163
  58.7 0.1 select_convert_fusion
  58.8 1.9 %collective-permute-start.15 = (bf16[2,128,512]{2,1,0:T(8,128)(2,1)S(1)}, bf16[2,128,512]{2,1,0:T(8,128)(2,1)S(1)}, u32[]{:S(2)}, u32[]{:S(2)}) collective-permute-start(bf16[2,128,512]{2,1,0:T(8,128)(2,1)S(1)} %copy-done.14), channel_id=1, source_target_pairs={{2,6},{4,0},{6,10},{8,4},{10,14},{12,8},{14,18},{16,12},{18,22},{2... | collective-permute-start | bytes 786440 | tf_op jit(solution)/shard_map/ppermute | solution.py:121
  60.8 0.1 add_convert_fusion.4
  60.9 4.3 %collective-permute-start.13 = (bf16[2,128,512]{2,1,0:T(8,128)(2,1)S(1)}, bf16[2,128,512]{2,1,0:T(8,128)(2,1)S(1)}, u32[]{:S(2)}, u32[]{:S(2)}) collective-permute-start(bf16[2,128,512]{2,1,0:T(8,128)(2,1)S(1)} %add_convert_fusion.4), channel_id=1, source_target_pairs={{6,2},{0,4},{10,6},{4,8},{14,10},{8,12},{18,14},{12,16},{22,18},{1... | collective-permute-start | bytes 786440 | tf_op jit(solution)/shard_map/ppermute | solution.py:121
  65.1 0.1 add_convert_fusion.2
  65.2 1.9 %collective-permute-start.17 = (bf16[2,128,512]{2,1,0:T(8,128)(2,1)S(1)}, bf16[2,128,512]{2,1,0:T(8,128)(2,1)S(1)}, u32[]{:S(2)}, u32[]{:S(2)}) collective-permute-start(bf16[2,128,512]{2,1,0:T(8,128)(2,1)S(1)} %add_convert_fusion.2), channel_id=1, source_target_pairs={{6,2},{0,4},{10,6},{4,8},{14,10},{8,12},{18,14},{12,16},{22,18},{1... | collective-permute-start | bytes 786440 | tf_op jit(solution)/shard_map/ppermute | solution.py:121
  67.2 0.7 pad_maximum_fusion.3
  67.9 0.3 collective-permute-start.9
  68.2 10.1 %collective-permute-done.13 = bf16[2,128,512]{2,1,0:T(8,128)(2,1)S(1)} collective-permute-done((bf16[2,128,512]{2,1,0:T(8,128)(2,1)S(1)}, bf16[2,128,512]{2,1,0:T(8,128)(2,1)S(1)}, u32[]{:S(2)}, u32[]{:S(2)}) %collective-permute-start.13) | collective-permute-done | bytes 262176 | tf_op jit(solution)/shard_map/ppermute | solution.py:121
  78.2 0.1 add_convert_fusion.3
  78.4 2.6 %collective-permute-done.17 = bf16[2,128,512]{2,1,0:T(8,128)(2,1)S(1)} collective-permute-done((bf16[2,128,512]{2,1,0:T(8,128)(2,1)S(1)}, bf16[2,128,512]{2,1,0:T(8,128)(2,1)S(1)}, u32[]{:S(2)}, u32[]{:S(2)}) %collective-permute-start.17) | collective-permute-done | bytes 262176 | tf_op jit(solution)/shard_map/ppermute | solution.py:121
  81.0 0.1 add_convert_fusion.1
  81.2 0.8 %fusion.5 = (bf16[128,1024]{1,0:T(8,128)(2,1)}, bf16[128,1024]{1,0:T(8,128)(2,1)}) fusion(bf16[2,128,512]{2,1,0:T(8,128)(2,1)S(1)} %add_convert_fusion.1, bf16[2,128,512]{2,1,0:T(8,128)(2,1)S(1)} %add_convert_fusion.3), kind=kLoop, calls=%fused_computation.17 | loop fusion | flops 1048576 | bytes 1048576 | tf_op jit(solution)/shard_map/squeeze | solution.py:174
  82.0 1.0 %add_convert_fusion = bf16[128,2048]{1,0:T(8,128)(2,1)} fusion(bf16[128,2048]{1,0:T(8,128)(2,1)S(1)} %collective-permute-done.9, f32[128,4096]{1,0:T(8,128)S(1)} %fusion.6, pred[]{:T(512)S(6)} %eq.3), kind=kLoop, calls=%fused_computation.4 | loop fusion | flops 1048576 | bytes 3145729 | tf_op jit(solution)/shard_map/convert_element_type | solution.py:168
  (44 shorter events, 0.2 us)
Async XLA Ops:
  0.6 18.9 %collective-permute-start = (bf16[128,2048]{1,0:T(8,128)(2,1)}, bf16[128,2048]{1,0:T(8,128)(2,1)S(1)}, u32[]{:S(2)}, u32[]{:S(2)}) collective-permute-start(bf16[128,2048]{1,0:T(8,128)(2,1)} %param.11), channel_id=1, source_target_pairs={{0,1},{1,0},{2,3},{3,2},{4,5},{5,4},{6,7},{7,6},{8,9},{9,8},{10,11... | collective-permute-start | bytes 1572872 | tf_op jit(solution)/shard_map/ppermute | solution.py:128
  3.1 30.5 %copy-start.5 = (bf16[2,128,512]{2,1,0:T(8,128)(2,1)}, bf16[2,128,512]{2,1,0:T(8,128)(2,1)S(1)}, u32[]{:S(2)}) copy-start(bf16[2,128,512]{2,1,0:T(8,128)(2,1)S(1)} %pad_maximum_fusion.1.own_ref) | copy-start | bytes 786436
  3.1 13.7 %collective-permute-start.1 = (bf16[2,128,512]{2,1,0:T(8,128)(2,1)S(1)}, bf16[2,128,512]{2,1,0:T(8,128)(2,1)S(1)}, u32[]{:S(2)}, u32[]{:S(2)}) collective-permute-start(bf16[2,128,512]{2,1,0:T(8,128)(2,1)S(1)} %pad_maximum_fusion.1.own_ref), channel_id=1, source_target_pairs={{2,6},{4,0},{6,10},{8,4},{10,14},{12,8},{14,18},{16,12},{18,22},{2... | collective-permute-start | bytes 786440 | tf_op jit(solution)/shard_map/ppermute | solution.py:121
  6.2 26.8 %collective-permute-start.2 = (bf16[2,128,512]{2,1,0:T(8,128)(2,1)S(1)}, bf16[2,128,512]{2,1,0:T(8,128)(2,1)S(1)}, u32[]{:S(2)}, u32[]{:S(2)}) collective-permute-start(bf16[2,128,512]{2,1,0:T(8,128)(2,1)S(1)} %pad_maximum_fusion.1.own_ref), channel_id=1, source_target_pairs={{6,2},{0,4},{10,6},{4,8},{14,10},{8,12},{18,14},{12,16},{22,18},{1... | collective-permute-start | bytes 786440 | tf_op jit(solution)/shard_map/ppermute | solution.py:121
  9.3 24.2 %collective-permute-start.3 = (bf16[2,128,512]{2,1,0:T(8,128)(2,1)S(1)}, bf16[2,128,512]{2,1,0:T(8,128)(2,1)S(1)}, u32[]{:S(2)}, u32[]{:S(2)}) collective-permute-start(bf16[2,128,512]{2,1,0:T(8,128)(2,1)S(1)} %pad_maximum_fusion.1.own_ref), channel_id=1, source_target_pairs={{0,2},{2,0},{4,6},{6,4},{8,10},{10,8},{12,14},{14,12},{16,18},{18,... | collective-permute-start | bytes 786440 | tf_op jit(solution)/shard_map/ppermute | solution.py:121
  10.0 30.4 %copy-start.4 = (bf16[2,128,512]{2,1,0:T(8,128)(2,1)}, bf16[2,128,512]{2,1,0:T(8,128)(2,1)S(1)}, u32[]{:S(2)}) copy-start(bf16[2,128,512]{2,1,0:T(8,128)(2,1)S(1)} %pad_maximum_fusion.2.own_ref) | copy-start | bytes 786436
  10.0 23.0 %collective-permute-start.5 = (bf16[2,128,512]{2,1,0:T(8,128)(2,1)S(1)}, bf16[2,128,512]{2,1,0:T(8,128)(2,1)S(1)}, u32[]{:S(2)}, u32[]{:S(2)}) collective-permute-start(bf16[2,128,512]{2,1,0:T(8,128)(2,1)S(1)} %pad_maximum_fusion.2.own_ref), channel_id=1, source_target_pairs={{2,6},{4,0},{6,10},{8,4},{10,14},{12,8},{14,18},{16,12},{18,22},{2... | collective-permute-start | bytes 786440 | tf_op jit(solution)/shard_map/ppermute | solution.py:121
  16.7 16.8 %copy-start.10 = (bf16[2,128,512]{2,1,0:T(8,128)(2,1)}, bf16[2,128,512]{2,1,0:T(8,128)(2,1)S(1)}, u32[]{:S(2)}) copy-start(bf16[2,128,512]{2,1,0:T(8,128)(2,1)S(1)} %collective-permute-done.1.a_ref) | copy-start | bytes 786436
  16.7 24.3 %collective-permute-start.6 = (bf16[2,128,512]{2,1,0:T(8,128)(2,1)S(1)}, bf16[2,128,512]{2,1,0:T(8,128)(2,1)S(1)}, u32[]{:S(2)}, u32[]{:S(2)}) collective-permute-start(bf16[2,128,512]{2,1,0:T(8,128)(2,1)S(1)} %pad_maximum_fusion.2.own_ref), channel_id=1, source_target_pairs={{6,2},{0,4},{10,6},{4,8},{14,10},{8,12},{18,14},{12,16},{22,18},{1... | collective-permute-start | bytes 786440 | tf_op jit(solution)/shard_map/ppermute | solution.py:121
  19.6 14.0 %collective-permute-start.4 = (bf16[2,128,512]{2,1,0:T(8,128)(2,1)S(1)}, bf16[2,128,512]{2,1,0:T(8,128)(2,1)S(1)}, u32[]{:S(2)}, u32[]{:S(2)}) collective-permute-start(bf16[2,128,512]{2,1,0:T(8,128)(2,1)S(1)} %collective-permute-done.1.a_ref), channel_id=1, source_target_pairs={{0,2},{2,0},{4,6},{6,4},{8,10},{10,8},{12,14},{14,12},{16,18},{18,... | collective-permute-start | bytes 786440 | tf_op jit(solution)/shard_map/ppermute | solution.py:121
  33.0 0.7 copy-start.11
  33.0 12.7 %collective-permute-start.7 = (bf16[2,128,512]{2,1,0:T(8,128)(2,1)S(1)}, bf16[2,128,512]{2,1,0:T(8,128)(2,1)S(1)}, u32[]{:S(2)}, u32[]{:S(2)}) collective-permute-start(bf16[2,128,512]{2,1,0:T(8,128)(2,1)S(1)} %pad_maximum_fusion.2.own_ref), channel_id=1, source_target_pairs={{0,2},{2,0},{4,6},{6,4},{8,10},{10,8},{12,14},{14,12},{16,18},{18,... | collective-permute-start | bytes 786440 | tf_op jit(solution)/shard_map/ppermute | solution.py:121
  33.0 12.7 %copy-start.9 = (bf16[2,128,512]{2,1,0:T(8,128)(2,1)}, bf16[2,128,512]{2,1,0:T(8,128)(2,1)S(1)}, u32[]{:S(2)}) copy-start(bf16[2,128,512]{2,1,0:T(8,128)(2,1)S(1)} %collective-permute-done.5.a_ref) | copy-start | bytes 786436
  33.0 12.7 %collective-permute-start.8 = (bf16[2,128,512]{2,1,0:T(8,128)(2,1)S(1)}, bf16[2,128,512]{2,1,0:T(8,128)(2,1)S(1)}, u32[]{:S(2)}, u32[]{:S(2)}) collective-permute-start(bf16[2,128,512]{2,1,0:T(8,128)(2,1)S(1)} %collective-permute-done.5.a_ref), channel_id=1, source_target_pairs={{0,2},{2,0},{4,6},{6,4},{8,10},{10,8},{12,14},{14,12},{16,18},{18,... | collective-permute-start | bytes 786440 | tf_op jit(solution)/shard_map/ppermute | solution.py:121
  33.5 0.7 copy-start.12
  33.5 0.8 copy-start.17
  40.4 13.4 %copy-start.6 = (bf16[128,512]{1,0:T(8,128)(2,1)S(1)}, bf16[128,512]{1,0:T(8,128)(2,1)}, u32[]{:S(2)}) copy-start(bf16[128,512]{1,0:T(8,128)(2,1)} %get-tuple-element.18) | copy-start | bytes 393220
  40.5 18.4 %collective-permute-start.12 = (bf16[2,128,512]{2,1,0:T(8,128)(2,1)}, bf16[2,128,512]{2,1,0:T(8,128)(2,1)S(1)}, u32[]{:S(2)}, u32[]{:S(2)}) collective-permute-start(bf16[2,128,512]{2,1,0:T(8,128)(2,1)} %get-tuple-element.26), channel_id=1, source_target_pairs={{0,2},{2,0},{4,6},{6,4},{8,10},{10,8},{12,14},{14,12},{16,18},{18,... | collective-permute-start | bytes 786440 | tf_op jit(solution)/shard_map/ppermute | solution.py:121
  40.6 24.6 %collective-permute-start.10 = (bf16[2,128,512]{2,1,0:T(8,128)(2,1)}, bf16[2,128,512]{2,1,0:T(8,128)(2,1)S(1)}, u32[]{:S(2)}, u32[]{:S(2)}) collective-permute-start(bf16[2,128,512]{2,1,0:T(8,128)(2,1)} %get-tuple-element.23), channel_id=1, source_target_pairs={{0,2},{2,0},{4,6},{6,4},{8,10},{10,8},{12,14},{14,12},{16,18},{18,... | collective-permute-start | bytes 786440 | tf_op jit(solution)/shard_map/ppermute | solution.py:121
  41.0 4.7 %copy-start.13 = (bf16[2,128,512]{2,1,0:T(8,128)(2,1)}, bf16[2,128,512]{2,1,0:T(8,128)(2,1)S(1)}, u32[]{:S(2)}) copy-start(bf16[2,128,512]{2,1,0:T(8,128)(2,1)S(1)} %collective-permute-done.6.b_ref) | copy-start | bytes 786436
  41.0 26.9 %collective-permute-start.11 = (bf16[2,128,512]{2,1,0:T(8,128)(2,1)}, bf16[2,128,512]{2,1,0:T(8,128)(2,1)S(1)}, u32[]{:S(2)}, u32[]{:S(2)}) collective-permute-start(bf16[2,128,512]{2,1,0:T(8,128)(2,1)} %get-tuple-element.24), channel_id=1, source_target_pairs={{2,6},{4,0},{6,10},{8,4},{10,14},{12,8},{14,18},{16,12},{18,22},{2... | collective-permute-start | bytes 786440 | tf_op jit(solution)/shard_map/ppermute | solution.py:121
  45.7 0.7 copy-start.15
  46.4 0.7 copy-start.16
  53.3 5.6 %copy-start.14 = (bf16[2,128,512]{2,1,0:T(8,128)(2,1)S(1)}, bf16[2,128,512]{2,1,0:T(8,128)(2,1)}, u32[]{:S(2)}) copy-start(bf16[2,128,512]{2,1,0:T(8,128)(2,1)} %get-tuple-element.29) | copy-start | bytes 786436
  53.3 7.5 %copy-start.2 = (bf16[2,128,512]{2,1,0:T(8,128)(2,1)S(1)}, bf16[2,128,512]{2,1,0:T(8,128)(2,1)}, u32[]{:S(2)}) copy-start(bf16[2,128,512]{2,1,0:T(8,128)(2,1)} %get-tuple-element.25) | copy-start | bytes 786436
  53.3 7.6 %collective-permute-start.16 = (bf16[2,128,512]{2,1,0:T(8,128)(2,1)}, bf16[2,128,512]{2,1,0:T(8,128)(2,1)S(1)}, u32[]{:S(2)}, u32[]{:S(2)}) collective-permute-start(bf16[2,128,512]{2,1,0:T(8,128)(2,1)} %get-tuple-element.31), channel_id=1, source_target_pairs={{0,2},{2,0},{4,6},{6,4},{8,10},{10,8},{12,14},{14,12},{16,18},{18,... | collective-permute-start | bytes 786440 | tf_op jit(solution)/shard_map/ppermute | solution.py:121
  53.6 24.7 %collective-permute-start.14 = (bf16[2,128,512]{2,1,0:T(8,128)(2,1)}, bf16[2,128,512]{2,1,0:T(8,128)(2,1)S(1)}, u32[]{:S(2)}, u32[]{:S(2)}) collective-permute-start(bf16[2,128,512]{2,1,0:T(8,128)(2,1)} %get-tuple-element.28), channel_id=1, source_target_pairs={{0,2},{2,0},{4,6},{6,4},{8,10},{10,8},{12,14},{14,12},{16,18},{18,... | collective-permute-start | bytes 786440 | tf_op jit(solution)/shard_map/ppermute | solution.py:121
  53.9 11.3 %copy-start.3 = (bf16[2,128,512]{2,1,0:T(8,128)(2,1)S(1)}, bf16[2,128,512]{2,1,0:T(8,128)(2,1)}, u32[]{:S(2)}) copy-start(bf16[2,128,512]{2,1,0:T(8,128)(2,1)} %get-tuple-element.30) | copy-start | bytes 786436
  53.9 13.3 %copy-start.7 = (bf16[128,512]{1,0:T(8,128)(2,1)S(1)}, bf16[128,512]{1,0:T(8,128)(2,1)}, u32[]{:S(2)}) copy-start(bf16[128,512]{1,0:T(8,128)(2,1)} %get-tuple-element.20) | copy-start | bytes 393220
  53.9 13.3 %copy-start.8 = (bf16[128,512]{1,0:T(8,128)(2,1)S(1)}, bf16[128,512]{1,0:T(8,128)(2,1)}, u32[]{:S(2)}) copy-start(bf16[128,512]{1,0:T(8,128)(2,1)} %get-tuple-element.21) | copy-start | bytes 393220
  53.9 24.3 %copy-start = (bf16[2,128,512]{2,1,0:T(8,128)(2,1)S(1)}, bf16[2,128,512]{2,1,0:T(8,128)(2,1)}, u32[]{:S(2)}) copy-start(bf16[2,128,512]{2,1,0:T(8,128)(2,1)} %get-tuple-element.22) | copy-start | bytes 786436
  53.9 27.1 %copy-start.1 = (bf16[2,128,512]{2,1,0:T(8,128)(2,1)S(1)}, bf16[2,128,512]{2,1,0:T(8,128)(2,1)}, u32[]{:S(2)}) copy-start(bf16[2,128,512]{2,1,0:T(8,128)(2,1)} %get-tuple-element.27) | copy-start | bytes 786436
  58.8 19.5 %collective-permute-start.15 = (bf16[2,128,512]{2,1,0:T(8,128)(2,1)S(1)}, bf16[2,128,512]{2,1,0:T(8,128)(2,1)S(1)}, u32[]{:S(2)}, u32[]{:S(2)}) collective-permute-start(bf16[2,128,512]{2,1,0:T(8,128)(2,1)S(1)} %copy-done.14), channel_id=1, source_target_pairs={{2,6},{4,0},{6,10},{8,4},{10,14},{12,8},{14,18},{16,12},{18,22},{2... | collective-permute-start | bytes 786440 | tf_op jit(solution)/shard_map/ppermute | solution.py:121
  60.9 17.4 %collective-permute-start.13 = (bf16[2,128,512]{2,1,0:T(8,128)(2,1)S(1)}, bf16[2,128,512]{2,1,0:T(8,128)(2,1)S(1)}, u32[]{:S(2)}, u32[]{:S(2)}) collective-permute-start(bf16[2,128,512]{2,1,0:T(8,128)(2,1)S(1)} %add_convert_fusion.4), channel_id=1, source_target_pairs={{6,2},{0,4},{10,6},{4,8},{14,10},{8,12},{18,14},{12,16},{22,18},{1... | collective-permute-start | bytes 786440 | tf_op jit(solution)/shard_map/ppermute | solution.py:121
  65.2 15.8 %collective-permute-start.17 = (bf16[2,128,512]{2,1,0:T(8,128)(2,1)S(1)}, bf16[2,128,512]{2,1,0:T(8,128)(2,1)S(1)}, u32[]{:S(2)}, u32[]{:S(2)}) collective-permute-start(bf16[2,128,512]{2,1,0:T(8,128)(2,1)S(1)} %add_convert_fusion.2), channel_id=1, source_target_pairs={{6,2},{0,4},{10,6},{4,8},{14,10},{8,12},{18,14},{12,16},{22,18},{1... | collective-permute-start | bytes 786440 | tf_op jit(solution)/shard_map/ppermute | solution.py:121
  67.9 14.1 %collective-permute-start.9 = (bf16[128,2048]{1,0:T(8,128)(2,1)S(1)}, bf16[128,2048]{1,0:T(8,128)(2,1)S(1)}, u32[]{:S(2)}, u32[]{:S(2)}) collective-permute-start(bf16[128,2048]{1,0:T(8,128)(2,1)S(1)} %select_convert_fusion), channel_id=1, source_target_pairs={{0,1},{1,0},{2,3},{3,2},{4,5},{5,4},{6,7},{7,6},{8,9},{9,8},{10,11... | collective-permute-start | bytes 1572872 | tf_op jit(solution)/shard_map/ppermute | solution.py:167
where the time goes:
time: 83.9 us; the launch traced here: 83 us
  starting transfers between devices  35 us (42%)
  waiting for transfers between devices  12.7 us (15%)
  Pallas kernels  12.3 us (15%)
  matrix products  11.8 us (14%)
  other arithmetic  6.2 us (7%)
  local copies, waits for them, and re-layouts  4.04 us (5%)
  between operations  1 us (1%)
    ppermute x16, starting transfers between devices, move(): return lax.ppermute(x, 'ctx', pairs)  33.5 us
    ppermute x16, waiting for transfers between devices, move(): return lax.ppermute(x, 'ctx', pairs)  12.7 us
    pallas_call x2, Pallas kernels, attend(): pl.pallas_call(functools.partial(attend_kernel, rows, total, factor, firs...  12.3 us
    dot_general x1, matrix products, per_device(): lax.dot_general(grad_full, out_weight, (((1,), (1,)), ((), ())), preferre...  6.96 us
    dot_general x1, matrix products, per_device(): partial = jnp.dot(attention, out_weight, preferred_element_type=f32)  4.8 us
    unnamed x36, local copies, waits for them, and re-layouts  2.18 us
  transfers between devices with their start and end apart: 18, of which 2 were waited for; matrix products, arithmetic and copies ran while one was open for 23% of the time, Pallas kernels for 15%

commit v1 on v0

--- a/solution.py
+++ b/solution.py
@@ -13,7 +13,7 @@
 
 
 def attend_kernel(
-    row_count, total, factor, first, index_ref, bound_ref, inv_ref,
+    row_count, total, factor, first, index_ref, length_ref, dilation_ref,
     q_ref, go_ref, own_ref, a_ref, b_ref, po_ref, pa_ref,
     att_ref, gq_ref, own_t, a_t, b_t, po_t, pa_t, dist,
 ):
@@ -24,12 +24,14 @@
     def _():
         me = index_ref[0]
         sign = 1 - 2 * lax.rem(me, 2)
-        ndocs = bound_ref.shape[0]
+        ends = [length_ref[0]]
+        for n in range(1, length_ref.shape[0]):
+            ends.append(ends[-1] + length_ref[n])
 
         def segment(pos):
             seg = jnp.zeros(pos.shape, jnp.int32)
-            for n in range(ndocs):
-                seg = seg + (pos >= bound_ref[n]).astype(jnp.int32)
+            for end in ends:
+                seg = seg + (pos >= end).astype(jnp.int32)
             return seg
 
         qpos = me * row_count + lax.broadcasted_iota(jnp.int32, (1, row_count), 1)
@@ -42,7 +44,8 @@
             gap = jnp.abs(kpos - qpos).astype(jnp.float32)
             dist[pl.ds(i * row_count, row_count), :] = jnp.where(same, gap, FAR)
 
-    inv = inv_ref[first + pl.program_id(0)]
+    spacing = jnp.full((1, row_count), dilation_ref[first + pl.program_id(0)], jnp.int32)
+    inv = 1.0 / spacing.astype(jnp.float32)
     steps = dist[...] * inv
     whole = jnp.floor(steps + 0.5)
     mask = (whole <= HALF) & (jnp.abs(steps - whole) < 0.01)
@@ -73,7 +76,7 @@
         out[1] = vt[i * row_count : (i + 1) * row_count]
 
 
-def attend(index, bounds, inv, q, go, slabs, first, total, factor, width):
+def attend(index, lengths, dilation, q, go, slabs, first, total, factor, width):
     rows, cols = q.shape[0], slabs[0].shape[2]
     heads = cols // width
     smem = pl.BlockSpec(memory_space=pltpu.SMEM)
@@ -95,7 +98,7 @@
             bytes_accessed=24 * 2 * rows * cols,
             transcendentals=heads * 5 * rows * rows,
         ),
-    )(index, bounds, inv, q, go, *slabs)
+    )(index, lengths, dilation, q, go, *slabs)
 
 
 def per_device(queries, keys, values, out_weight, mixed_grad, lengths, dilation):
@@ -108,8 +111,6 @@
     total = rows * count
     assert 2 * rows >= HALF * MAXD and count % 2 == 0
     index = lax.axis_index("ctx").astype(jnp.int32).reshape(1)
-    bounds = jnp.cumsum(lengths).astype(jnp.int32)
-    inv = 1.0 / dilation.astype(jnp.float32)
 
     inward = [
         (j, t) for j in range(count) for t in [j - 2 if j % 2 == 0 else j + 2] if 0 <= t < count
@@ -120,7 +121,7 @@
     def move(x, pairs):
         return lax.ppermute(x, "ctx", pairs)
 
-    groups = 2 if local_heads % 2 == 0 else 1
+    groups = 1
     gh = local_heads // groups
     cut = [slice(g * gh * width, (g + 1) * gh * width) for g in range(groups)]
     half = mixed_grad.shape[1]
@@ -145,17 +146,16 @@
     f32 = jnp.float32
     for g in range(groups):
         att, gq, own_t, a_t, b_t, po_t, pa_t = attend(
-            index, bounds, inv, queries, grad_attention, stacks[g], g * gh, total, factor, width
+            index, lengths, dilation, queries, grad_attention, stacks[g], g * gh, total, factor, width
         )
         pa_back = move(pa_t, swapped)
         b_back = move(b_t, inward)
         po_back = move(po_t, swapped)
         a_sum = (a_t.astype(f32) + pa_back.astype(f32)).astype(jnp.bfloat16)
         a_back = move(a_sum, outward)
+        terms = (own_t, po_back, b_back, a_back)
         gkvs.append(
-            (
-                own_t.astype(f32) + po_back.astype(f32) + b_back.astype(f32) + a_back.astype(f32)
-            ).astype(jnp.bfloat16)
+            [sum(term[i].astype(f32) for term in terms).astype(jnp.bfloat16) for i in range(2)]
         )
         atts.append(att)
         gqs.append(gq)
@@ -170,8 +170,10 @@
         mixed = lax.psum_scatter(
             partial.astype(jnp.bfloat16), "head", scatter_dimension=1, tiled=True
         )
-    gkv = jnp.concatenate(gkvs, axis=2)
-    return mixed, jnp.concatenate(gqs, axis=1), gkv[0], gkv[1]
+    grad_keys, grad_values = (
+        jnp.concatenate([pair[i] for pair in gkvs], axis=1) for i in range(2)
+    )
+    return mixed, jnp.concatenate(gqs, axis=1), grad_keys, grad_values
 
 
 def solution(mesh):

time: 83.9 us -> 85.5 us (1.019)
  waiting for transfers between devices: 12.7 us -> 36.1 us
  starting transfers between devices: 35 us -> 20.2 us
  local copies, waits for them, and re-layouts: 4.04 us -> 1.12 us
  Pallas kernels: 12.3 us -> 10 us
  other arithmetic: 6.2 us -> 4.64 us
    ppermute x16 -> x8, waiting for transfers between devices: 12.7 us -> 31 us  [move(): return lax.ppermute(x, 'ctx', pairs)]
    ppermute x16 -> x8, starting transfers between devices: 33.5 us -> 17.7 us  [move(): return lax.ppermute(x, 'ctx', pairs)]
    ppermute x1, waiting for transfers between devices: 0.01 us -> 5.08 us  [per_device(): came = lax.ppermute(away, 'head', [(0, 1), (1, 0)])]
    pallas_call x2 -> x1, Pallas kernels: 12.3 us -> 10 us  [attend(): pl.pallas_call(functools.partial(attend_kernel, rows, total, factor, firs...]
    another operation x2 -> x0, local copies, waits for them, and re-layouts: 1.86 us -> none  [the longest x1 1.13 us: per_device(): own = jnp.stack([keys[:, cut[g]], values[:, cut[g]]])]
    div x1 -> x0, other arithmetic: 1.2 us -> none  [per_device(): inv = 1.0 / dilation.astype(jnp.float32)]
    add x0 -> x1, other arithmetic: none -> 1.15 us  [per_device(): sum((term[i].astype(f32) for term in terms)).astype(jnp.bfloat16)]
    unnamed x36 -> x18, local copies, waits for them, and re-layouts: 2.18 us -> 1.12 us
  transfers between devices with their start and end apart: 18 -> 10, of which waited for: 2 -> 4; matrix products, arithmetic and copies ran while one was open for 23% -> 17% of each run, Pallas kernels for 15% -> 0%
where the time goes in v1:
time: 85.5 us; the launch traced here: 84.7 us
  waiting for transfers between devices  36.1 us (42%)
  starting transfers between devices  20.2 us (24%)
  matrix products  11.8 us (14%)
  Pallas kernels  10 us (12%)
  other arithmetic  4.64 us (5%)
  local copies, waits for them, and re-layouts  1.12 us (1%)
    ppermute x8, waiting for transfers between devices, move(): return lax.ppermute(x, 'ctx', pairs)  31 us
    ppermute x8, starting transfers between devices, move(): return lax.ppermute(x, 'ctx', pairs)  17.7 us
    pallas_call x1, Pallas kernels, attend(): pl.pallas_call(functools.partial(attend_kernel, rows, total, factor, firs...  10 us
    dot_general x1, matrix products, per_device(): lax.dot_general(grad_full, out_weight, (((1,), (1,)), ((), ())), preferre...  6.96 us
    ppermute x1, waiting for transfers between devices, per_device(): came = lax.ppermute(away, 'head', [(0, 1), (1, 0)])  5.08 us
    dot_general x1, matrix products, per_device(): partial = jnp.dot(attention, out_weight, preferred_element_type=f32)  4.86 us
  transfers between devices with their start and end apart: 10, of which 4 were waited for; matrix products, arithmetic and copies ran while one was open for 17% of the time, Pallas kernels for 0%

profile of v1, /device:TPU:9, one launch (start us, length us, event | category | flops | bytes accessed | tf_op | source)
XLA Modules:
  0.0 84.7 jit_solution(16052982762166812271)
XLA Ops:
  0.6 1.1 %pad_maximum_fusion.own_ref = bf16[2,128,1024]{2,1,0:T(8,128)(2,1)S(1)} fusion(bf16[1,128,1024]{2,1,0:T(8,128)(2,1)} %bitcast.10, bf16[1,128,1024]{2,1,0:T(8,128)(2,1)} %bitcast.11), kind=kLoop, calls=%fused_computation.7 | loop fusion | flops 262144 | bytes 1048576 | tf_op jit(solution)/shard_map/stack | solution.py:138
  1.7 0.0 copy-start.2
  1.7 3.1 %collective-permute-start.1 = (bf16[2,128,1024]{2,1,0:T(8,128)(2,1)S(1)}, bf16[2,128,1024]{2,1,0:T(8,128)(2,1)S(1)}, u32[]{:S(2)}, u32[]{:S(2)}) collective-permute-start(bf16[2,128,1024]{2,1,0:T(8,128)(2,1)S(1)} %pad_maximum_fusion.own_ref), channel_id=1, source_target_pairs={{2,6},{4,0},{6,10},{8,4},{10,14},{12,8},{14,18},{16,12},{18,22},{2... | collective-permute-start | bytes 1572872 | tf_op jit(solution)/shard_map/ppermute | solution.py:122
  4.9 1.3 %collective-permute-start = (bf16[128,2048]{1,0:T(8,128)(2,1)}, bf16[128,2048]{1,0:T(8,128)(2,1)S(1)}, u32[]{:S(2)}, u32[]{:S(2)}) collective-permute-start(bf16[128,2048]{1,0:T(8,128)(2,1)} %param.11), channel_id=1, source_target_pairs={{0,1},{1,0},{2,3},{3,2},{4,5},{5,4},{6,7},{7,6},{8,9},{9,8},{10,11... | collective-permute-start | bytes 1572872 | tf_op jit(solution)/shard_map/ppermute | solution.py:129
  6.2 1.1 %collective-permute-start.3 = (bf16[2,128,1024]{2,1,0:T(8,128)(2,1)S(1)}, bf16[2,128,1024]{2,1,0:T(8,128)(2,1)S(1)}, u32[]{:S(2)}, u32[]{:S(2)}) collective-permute-start(bf16[2,128,1024]{2,1,0:T(8,128)(2,1)S(1)} %pad_maximum_fusion.own_ref), channel_id=1, source_target_pairs={{0,2},{2,0},{4,6},{6,4},{8,10},{10,8},{12,14},{14,12},{16,18},{18,... | collective-permute-start | bytes 1572872 | tf_op jit(solution)/shard_map/ppermute | solution.py:122
  7.3 2.1 %collective-permute-start.2 = (bf16[2,128,1024]{2,1,0:T(8,128)(2,1)S(1)}, bf16[2,128,1024]{2,1,0:T(8,128)(2,1)S(1)}, u32[]{:S(2)}, u32[]{:S(2)}) collective-permute-start(bf16[2,128,1024]{2,1,0:T(8,128)(2,1)S(1)} %pad_maximum_fusion.own_ref), channel_id=1, source_target_pairs={{6,2},{0,4},{10,6},{4,8},{14,10},{8,12},{18,14},{12,16},{22,18},{1... | collective-permute-start | bytes 1572872 | tf_op jit(solution)/shard_map/ppermute | solution.py:122
  9.4 16.3 %collective-permute-done.1.a_ref = bf16[2,128,1024]{2,1,0:T(8,128)(2,1)S(1)} collective-permute-done((bf16[2,128,1024]{2,1,0:T(8,128)(2,1)S(1)}, bf16[2,128,1024]{2,1,0:T(8,128)(2,1)S(1)}, u32[]{:S(2)}, u32[]{:S(2)}) %collective-permute-start.1) | collective-permute-done | bytes 524320 | tf_op jit(solution)/shard_map/ppermute | solution.py:122
  25.7 0.0 copy-start.3
  25.7 4.3 %collective-permute-start.4 = (bf16[2,128,1024]{2,1,0:T(8,128)(2,1)S(1)}, bf16[2,128,1024]{2,1,0:T(8,128)(2,1)S(1)}, u32[]{:S(2)}, u32[]{:S(2)}) collective-permute-start(bf16[2,128,1024]{2,1,0:T(8,128)(2,1)S(1)} %collective-permute-done.1.a_ref), channel_id=1, source_target_pairs={{0,2},{2,0},{4,6},{6,4},{8,10},{10,8},{12,14},{14,12},{16,18},{18,... | collective-permute-start | bytes 1572872 | tf_op jit(solution)/shard_map/ppermute | solution.py:122
  30.0 0.0 collective-permute-done
  30.0 1.1 %broadcast_select_fusion.1 = (bf16[128,2048]{1,0:T(8,128)(2,1)S(1)}, bf16[128,2048]{1,0:T(8,128)(2,1)S(1)}) fusion(bf16[128,2048]{1,0:T(8,128)(2,1)} %param.11, bf16[128,2048]{1,0:T(8,128)(2,1)S(1)} %collective-permute-done, pred[]{:T(512)S(6)} %eq.3), kind=kLoop, calls=%fused_computation.11 | loop fusion | flops 524288 | bytes 2097153 | tf_op jit(solution)/shard_map/jit(_where)/select_n | solution.py:132
  31.1 7.0 %convolution_convert_fusion.go_ref = bf16[128,1024]{1,0:T(8,128)(2,1)} fusion(bf16[1024,4096]{1,0:T(8,128)(2,1)} %param.10, bf16[128,2048]{1,0:T(8,128)(2,1)S(1)} %get-tuple-element.21, bf16[128,2048]{1,0:T(8,128)(2,1)S(1)} %get-tuple-element.20), kind=kOutput, calls=%fused_computation | convolution fusion | flops 1075970048 | bytes 9699328 | tf_op jit(solution)/shard_map/dot_general | solution.py:141
  38.1 0.0 collective-permute-done.3.po_ref
  38.1 0.0 copy-start.4
  38.1 0.0 collective-permute-done.2.b_ref
  38.1 0.0 copy-start.5
  38.1 0.0 collective-permute-done.4.pa_ref
  38.1 0.0 copy-start.8
  38.1 0.0 copy-done.2
  38.1 0.0 copy-done.3
  38.1 0.7 copy-done.4
  38.9 0.2 copy-done.5
  39.1 0.2 copy-done.8
  39.2 10.0 %shard_map.102 = (bf16[128,1024]{1,0:T(8,128)(2,1)}, bf16[128,1024]{1,0:T(8,128)(2,1)}, bf16[2,128,1024]{2,1,0:T(8,128)(2,1)}, bf16[2,128,1024]{2,1,0:T(8,128)(2...) custom-call(s32[1]{0:T(128)} %bitcast.index_ref, s32[16]{0:T(128)} %length_ref.1, ...), custom_call_target="tpu_custom_call" | custom-call | flops 8053063680 | bytes 6291456 | tf_op jit(solution)/shard_map/pallas_call | solution.py:88
  49.3 0.0 copy-start.7
  49.3 0.0 copy-start.6
  49.3 0.0 copy-start.1
  49.3 0.3 collective-permute-start.8
  49.6 0.0 copy-start
  49.6 4.9 %fusion.6 = f32[128,4096]{1,0:T(8,128)S(1)} fusion(bf16[128,1024]{1,0:T(8,128)(2,1)} %get-tuple-element.11, bf16[1024,4096]{1,0:T(8,128)(2,1)} %param.10), kind=kOutput, calls=%fused_computation.15 | convolution fusion | flops 1073741824 | bytes 10747904 | tf_op jit(solution)/shard_map/dot_general | solution.py:163
  54.4 0.1 select_convert_fusion
  54.5 1.3 %collective-permute-start.5 = (bf16[128,2048]{1,0:T(8,128)(2,1)S(1)}, bf16[128,2048]{1,0:T(8,128)(2,1)S(1)}, u32[]{:S(2)}, u32[]{:S(2)}) collective-permute-start(bf16[128,2048]{1,0:T(8,128)(2,1)S(1)} %select_convert_fusion), channel_id=1, source_target_pairs={{0,1},{1,0},{2,3},{3,2},{4,5},{5,4},{6,7},{7,6},{8,9},{9,8},{10,11... | collective-permute-start | bytes 1572872 | tf_op jit(solution)/shard_map/ppermute | solution.py:167
  55.8 0.0 copy-done.7
  55.8 0.5 collective-permute-start.6
  56.3 0.0 copy-done.6
  56.4 1.9 %collective-permute-start.7 = (bf16[2,128,1024]{2,1,0:T(8,128)(2,1)S(1)}, bf16[2,128,1024]{2,1,0:T(8,128)(2,1)S(1)}, u32[]{:S(2)}, u32[]{:S(2)}) collective-permute-start(bf16[2,128,1024]{2,1,0:T(8,128)(2,1)S(1)} %copy-done.6), channel_id=1, source_target_pairs={{2,6},{4,0},{6,10},{8,4},{10,14},{12,8},{14,18},{16,12},{18,22},{2... | collective-permute-start | bytes 1572872 | tf_op jit(solution)/shard_map/ppermute | solution.py:122
  58.3 0.0 collective-permute-done.8
  58.3 0.0 copy-done.1
  58.3 0.2 add_convert_fusion
  58.5 4.3 %collective-permute-start.9 = (bf16[2,128,1024]{2,1,0:T(8,128)(2,1)S(1)}, bf16[2,128,1024]{2,1,0:T(8,128)(2,1)S(1)}, u32[]{:S(2)}, u32[]{:S(2)}) collective-permute-start(bf16[2,128,1024]{2,1,0:T(8,128)(2,1)S(1)} %add_convert_fusion), channel_id=1, source_target_pairs={{6,2},{0,4},{10,6},{4,8},{14,10},{8,12},{18,14},{12,16},{22,18},{1... | collective-permute-start | bytes 1572872 | tf_op jit(solution)/shard_map/ppermute | solution.py:122
  62.8 5.1 %collective-permute-done.5 = bf16[128,2048]{1,0:T(8,128)(2,1)S(1)} collective-permute-done((bf16[128,2048]{1,0:T(8,128)(2,1)S(1)}, bf16[128,2048]{1,0:T(8,128)(2,1)S(1)}, u32[]{:S(2)}, u32[]{:S(2)}) %collective-permute-start.5) | collective-permute-done | bytes 524320 | tf_op jit(solution)/shard_map/ppermute | solution.py:167
  67.8 1.0 %add_convert_fusion.1 = bf16[128,2048]{1,0:T(8,128)(2,1)} fusion(bf16[128,2048]{1,0:T(8,128)(2,1)S(1)} %collective-permute-done.5, f32[128,4096]{1,0:T(8,128)S(1)} %fusion.6, pred[]{:T(512)S(6)} %eq.3), kind=kLoop, calls=%fused_computation.5 | loop fusion | flops 1048576 | bytes 3145729 | tf_op jit(solution)/shard_map/convert_element_type | solution.py:168
  68.9 0.0 collective-permute-done.6
  68.9 11.1 %collective-permute-done.7 = bf16[2,128,1024]{2,1,0:T(8,128)(2,1)S(1)} collective-permute-done((bf16[2,128,1024]{2,1,0:T(8,128)(2,1)S(1)}, bf16[2,128,1024]{2,1,0:T(8,128)(2,1)S(1)}, u32[]{:S(2)}, u32[]{:S(2)}) %collective-permute-start.7) | collective-permute-done | bytes 524320 | tf_op jit(solution)/shard_map/ppermute | solution.py:122
  79.9 3.7 %collective-permute-done.9 = bf16[2,128,1024]{2,1,0:T(8,128)(2,1)S(1)} collective-permute-done((bf16[2,128,1024]{2,1,0:T(8,128)(2,1)S(1)}, bf16[2,128,1024]{2,1,0:T(8,128)(2,1)S(1)}, u32[]{:S(2)}, u32[]{:S(2)}) %collective-permute-start.9) | collective-permute-done | bytes 524320 | tf_op jit(solution)/shard_map/ppermute | solution.py:122
  83.6 0.0 copy-done
  83.6 1.1 %fusion.4 = (bf16[128,1024]{1,0:T(8,128)(2,1)}, bf16[128,1024]{1,0:T(8,128)(2,1)}) fusion(bf16[2,128,1024]{2,1,0:T(8,128)(2,1)S(1)} %collective-permute-done.9, bf16[2,128,1024]{2,1,0:T(8,128)(2,1)S(1)} %collective-permute-done.7, bf16[2,128,1024]{2,1,0:T(8,128)(2,1)S(1)} %collective-permute-done.6, bf16[2,128,1024]{2,1,0:T(8,128)(2,1)S(1)} %copy-done), kind=kLoop, calls=%fused_computation.13 | loop fusion | flops 2097152 | bytes 2621440 | tf_op jit(solution)/shard_map/add | solution.py:158
Async XLA Ops:
  1.7 36.4 %copy-start.2 = (bf16[2,128,1024]{2,1,0:T(8,128)(2,1)}, bf16[2,128,1024]{2,1,0:T(8,128)(2,1)S(1)}, u32[]{:S(2)}) copy-start(bf16[2,128,1024]{2,1,0:T(8,128)(2,1)S(1)} %pad_maximum_fusion.own_ref) | copy-start | bytes 1572868
  1.7 24.0 %collective-permute-start.1 = (bf16[2,128,1024]{2,1,0:T(8,128)(2,1)S(1)}, bf16[2,128,1024]{2,1,0:T(8,128)(2,1)S(1)}, u32[]{:S(2)}, u32[]{:S(2)}) collective-permute-start(bf16[2,128,1024]{2,1,0:T(8,128)(2,1)S(1)} %pad_maximum_fusion.own_ref), channel_id=1, source_target_pairs={{2,6},{4,0},{6,10},{8,4},{10,14},{12,8},{14,18},{16,12},{18,22},{2... | collective-permute-start | bytes 1572872 | tf_op jit(solution)/shard_map/ppermute | solution.py:122
  4.9 25.1 %collective-permute-start = (bf16[128,2048]{1,0:T(8,128)(2,1)}, bf16[128,2048]{1,0:T(8,128)(2,1)S(1)}, u32[]{:S(2)}, u32[]{:S(2)}) collective-permute-start(bf16[128,2048]{1,0:T(8,128)(2,1)} %param.11), channel_id=1, source_target_pairs={{0,1},{1,0},{2,3},{3,2},{4,5},{5,4},{6,7},{7,6},{8,9},{9,8},{10,11... | collective-permute-start | bytes 1572872 | tf_op jit(solution)/shard_map/ppermute | solution.py:129
  6.2 31.9 %collective-permute-start.3 = (bf16[2,128,1024]{2,1,0:T(8,128)(2,1)S(1)}, bf16[2,128,1024]{2,1,0:T(8,128)(2,1)S(1)}, u32[]{:S(2)}, u32[]{:S(2)}) collective-permute-start(bf16[2,128,1024]{2,1,0:T(8,128)(2,1)S(1)} %pad_maximum_fusion.own_ref), channel_id=1, source_target_pairs={{0,2},{2,0},{4,6},{6,4},{8,10},{10,8},{12,14},{14,12},{16,18},{18,... | collective-permute-start | bytes 1572872 | tf_op jit(solution)/shard_map/ppermute | solution.py:122
  7.3 30.8 %collective-permute-start.2 = (bf16[2,128,1024]{2,1,0:T(8,128)(2,1)S(1)}, bf16[2,128,1024]{2,1,0:T(8,128)(2,1)S(1)}, u32[]{:S(2)}, u32[]{:S(2)}) collective-permute-start(bf16[2,128,1024]{2,1,0:T(8,128)(2,1)S(1)} %pad_maximum_fusion.own_ref), channel_id=1, source_target_pairs={{6,2},{0,4},{10,6},{4,8},{14,10},{8,12},{18,14},{12,16},{22,18},{1... | collective-permute-start | bytes 1572872 | tf_op jit(solution)/shard_map/ppermute | solution.py:122
  25.7 12.4 %copy-start.3 = (bf16[2,128,1024]{2,1,0:T(8,128)(2,1)}, bf16[2,128,1024]{2,1,0:T(8,128)(2,1)S(1)}, u32[]{:S(2)}) copy-start(bf16[2,128,1024]{2,1,0:T(8,128)(2,1)S(1)} %collective-permute-done.1.a_ref) | copy-start | bytes 1572868
  25.7 12.4 %collective-permute-start.4 = (bf16[2,128,1024]{2,1,0:T(8,128)(2,1)S(1)}, bf16[2,128,1024]{2,1,0:T(8,128)(2,1)S(1)}, u32[]{:S(2)}, u32[]{:S(2)}) collective-permute-start(bf16[2,128,1024]{2,1,0:T(8,128)(2,1)S(1)} %collective-permute-done.1.a_ref), channel_id=1, source_target_pairs={{0,2},{2,0},{4,6},{6,4},{8,10},{10,8},{12,14},{14,12},{16,18},{18,... | collective-permute-start | bytes 1572872 | tf_op jit(solution)/shard_map/ppermute | solution.py:122
  38.1 0.8 copy-start.4
  38.1 1.0 %copy-start.5 = (bf16[2,128,1024]{2,1,0:T(8,128)(2,1)}, bf16[2,128,1024]{2,1,0:T(8,128)(2,1)S(1)}, u32[]{:S(2)}) copy-start(bf16[2,128,1024]{2,1,0:T(8,128)(2,1)S(1)} %collective-permute-done.2.b_ref) | copy-start | bytes 1572868
  38.1 1.1 %copy-start.8 = (bf16[2,128,1024]{2,1,0:T(8,128)(2,1)}, bf16[2,128,1024]{2,1,0:T(8,128)(2,1)S(1)}, u32[]{:S(2)}) copy-start(bf16[2,128,1024]{2,1,0:T(8,128)(2,1)S(1)} %collective-permute-done.4.pa_ref) | copy-start | bytes 1572868
  49.3 6.5 %copy-start.7 = (bf16[2,128,1024]{2,1,0:T(8,128)(2,1)S(1)}, bf16[2,128,1024]{2,1,0:T(8,128)(2,1)}, u32[]{:S(2)}) copy-start(bf16[2,128,1024]{2,1,0:T(8,128)(2,1)} %get-tuple-element.14) | copy-start | bytes 1572868
  49.3 7.1 %copy-start.6 = (bf16[2,128,1024]{2,1,0:T(8,128)(2,1)S(1)}, bf16[2,128,1024]{2,1,0:T(8,128)(2,1)}, u32[]{:S(2)}) copy-start(bf16[2,128,1024]{2,1,0:T(8,128)(2,1)} %get-tuple-element.15) | copy-start | bytes 1572868
  49.3 9.0 %copy-start.1 = (bf16[2,128,1024]{2,1,0:T(8,128)(2,1)S(1)}, bf16[2,128,1024]{2,1,0:T(8,128)(2,1)}, u32[]{:S(2)}) copy-start(bf16[2,128,1024]{2,1,0:T(8,128)(2,1)} %get-tuple-element.16) | copy-start | bytes 1572868
  49.3 9.0 %collective-permute-start.8 = (bf16[2,128,1024]{2,1,0:T(8,128)(2,1)}, bf16[2,128,1024]{2,1,0:T(8,128)(2,1)S(1)}, u32[]{:S(2)}, u32[]{:S(2)}) collective-permute-start(bf16[2,128,1024]{2,1,0:T(8,128)(2,1)} %get-tuple-element.17), channel_id=1, source_target_pairs={{0,2},{2,0},{4,6},{6,4},{8,10},{10,8},{12,14},{14,12},{16,18},{18,... | collective-permute-start | bytes 1572872 | tf_op jit(solution)/shard_map/ppermute | solution.py:122
  49.6 34.0 %copy-start = (bf16[2,128,1024]{2,1,0:T(8,128)(2,1)S(1)}, bf16[2,128,1024]{2,1,0:T(8,128)(2,1)}, u32[]{:S(2)}) copy-start(bf16[2,128,1024]{2,1,0:T(8,128)(2,1)} %get-tuple-element.13) | copy-start | bytes 1572868
  54.5 13.3 %collective-permute-start.5 = (bf16[128,2048]{1,0:T(8,128)(2,1)S(1)}, bf16[128,2048]{1,0:T(8,128)(2,1)S(1)}, u32[]{:S(2)}, u32[]{:S(2)}) collective-permute-start(bf16[128,2048]{1,0:T(8,128)(2,1)S(1)} %select_convert_fusion), channel_id=1, source_target_pairs={{0,1},{1,0},{2,3},{3,2},{4,5},{5,4},{6,7},{7,6},{8,9},{9,8},{10,11... | collective-permute-start | bytes 1572872 | tf_op jit(solution)/shard_map/ppermute | solution.py:167
  55.8 13.0 %collective-permute-start.6 = (bf16[2,128,1024]{2,1,0:T(8,128)(2,1)S(1)}, bf16[2,128,1024]{2,1,0:T(8,128)(2,1)S(1)}, u32[]{:S(2)}, u32[]{:S(2)}) collective-permute-start(bf16[2,128,1024]{2,1,0:T(8,128)(2,1)S(1)} %copy-done.7), channel_id=1, source_target_pairs={{0,2},{2,0},{4,6},{6,4},{8,10},{10,8},{12,14},{14,12},{16,18},{18,... | collective-permute-start | bytes 1572872 | tf_op jit(solution)/shard_map/ppermute | solution.py:122
  56.4 23.6 %collective-permute-start.7 = (bf16[2,128,1024]{2,1,0:T(8,128)(2,1)S(1)}, bf16[2,128,1024]{2,1,0:T(8,128)(2,1)S(1)}, u32[]{:S(2)}, u32[]{:S(2)}) collective-permute-start(bf16[2,128,1024]{2,1,0:T(8,128)(2,1)S(1)} %copy-done.6), channel_id=1, source_target_pairs={{2,6},{4,0},{6,10},{8,4},{10,14},{12,8},{14,18},{16,12},{18,22},{2... | collective-permute-start | bytes 1572872 | tf_op jit(solution)/shard_map/ppermute | solution.py:122
  58.5 25.1 %collective-permute-start.9 = (bf16[2,128,1024]{2,1,0:T(8,128)(2,1)S(1)}, bf16[2,128,1024]{2,1,0:T(8,128)(2,1)S(1)}, u32[]{:S(2)}, u32[]{:S(2)}) collective-permute-start(bf16[2,128,1024]{2,1,0:T(8,128)(2,1)S(1)} %add_convert_fusion), channel_id=1, source_target_pairs={{6,2},{0,4},{10,6},{4,8},{14,10},{8,12},{18,14},{12,16},{22,18},{1... | collective-permute-start | bytes 1572872 | tf_op jit(solution)/shard_map/ppermute | solution.py:122

commit v2 on v1

--- a/solution.py
+++ b/solution.py
@@ -136,14 +136,16 @@
     stacks = []
     for g in range(groups):
         own = jnp.stack([keys[:, cut[g]], values[:, cut[g]]])
-        a = move(own, inward)
-        stacks.append((own, a, move(own, outward), move(own, swapped), move(a, swapped)))
+        stacks.append([own, move(own, inward), move(own, outward), move(own, swapped)])
     grad_attention = lax.dot_general(
         grad_full, out_weight, (((1,), (1,)), ((), ())), preferred_element_type=jnp.float32
     ).astype(jnp.bfloat16)
 
     atts, gqs, gkvs = [], [], []
     f32 = jnp.float32
+    for slabs in stacks:
+        slabs[1], grad_attention = lax.optimization_barrier((slabs[1], grad_attention))
+        slabs.append(move(slabs[1], swapped))
     for g in range(groups):
         att, gq, own_t, a_t, b_t, po_t, pa_t = attend(
             index, lengths, dilation, queries, grad_attention, stacks[g], g * gh, total, factor, width
@@ -152,6 +154,7 @@
         b_back = move(b_t, inward)
         po_back = move(po_t, swapped)
         a_sum = (a_t.astype(f32) + pa_back.astype(f32)).astype(jnp.bfloat16)
+        a_sum, att = lax.optimization_barrier((a_sum, att))
         a_back = move(a_sum, outward)
         terms = (own_t, po_back, b_back, a_back)
         gkvs.append(

time: 85.5 us -> 82.5 us (0.965)
  starting transfers between devices: 20.2 us -> 16 us
  other arithmetic: 4.64 us -> 5.68 us
    ppermute x8, waiting for transfers between devices: 31 us -> 26.1 us  [move(): return lax.ppermute(x, 'ctx', pairs)]
    ppermute x1, waiting for transfers between devices: 0.01 us -> 4.4 us  [per_device(): other = lax.ppermute(mixed_grad, 'head', [(0, 1), (1, 0)])]
    ppermute x8, starting transfers between devices: 17.7 us -> 14.4 us  [move(): return lax.ppermute(x, 'ctx', pairs)]
    convert_element_type x1, other arithmetic: 0.19 us -> 1.24 us  [per_device(): a_sum = (a_t.astype(f32) + pa_back.astype(f32)).astype(jnp.bfloat16)]
    ppermute x1, starting transfers between devices: 1.27 us -> 0.32 us  [per_device(): came = lax.ppermute(away, 'head', [(0, 1), (1, 0)])]
    ppermute x1, waiting for transfers between devices: 5.08 us -> 6 us  [per_device(): came = lax.ppermute(away, 'head', [(0, 1), (1, 0)])]
  transfers between devices with their start and end apart: 10 -> 10, of which waited for: 4 -> 7; matrix products, arithmetic and copies ran while one was open for 17% -> 12% of each run, Pallas kernels for 0% -> 0%
where the time goes in v2:
time: 82.5 us; the launch traced here: 81.7 us
  waiting for transfers between devices  36.5 us (44%)
  starting transfers between devices  16 us (19%)
  matrix products  11.8 us (14%)
  Pallas kernels  10 us (12%)
  other arithmetic  5.68 us (7%)
  local copies, waits for them, and re-layouts  0.83 us (1%)
    ppermute x8, waiting for transfers between devices, move(): return lax.ppermute(x, 'ctx', pairs)  26.1 us
    ppermute x8, starting transfers between devices, move(): return lax.ppermute(x, 'ctx', pairs)  14.4 us
    pallas_call x1, Pallas kernels, attend(): pl.pallas_call(functools.partial(attend_kernel, rows, total, factor, firs...  10 us
    dot_general x1, matrix products, per_device(): lax.dot_general(grad_full, out_weight, (((1,), (1,)), ((), ())), preferre...  6.96 us
    ppermute x1, waiting for transfers between devices, per_device(): came = lax.ppermute(away, 'head', [(0, 1), (1, 0)])  6 us
    dot_general x1, matrix products, per_device(): partial = jnp.dot(attention, out_weight, preferred_element_type=f32)  4.83 us
    ppermute x1, waiting for transfers between devices, per_device(): other = lax.ppermute(mixed_grad, 'head', [(0, 1), (1, 0)])  4.4 us
  transfers between devices with their start and end apart: 10, of which 7 were waited for; matrix products, arithmetic and copies ran while one was open for 12% of the time, Pallas kernels for 0%

profile of v2, /device:TPU:9, one launch (start us, length us, event | category | flops | bytes accessed | tf_op | source)
XLA Modules:
  0.0 81.7 jit_solution(16641893389574561125)
XLA Ops:
  0.6 1.3 %collective-permute-start.1 = (bf16[128,2048]{1,0:T(8,128)(2,1)}, bf16[128,2048]{1,0:T(8,128)(2,1)S(1)}, u32[]{:S(2)}, u32[]{:S(2)}) collective-permute-start(bf16[128,2048]{1,0:T(8,128)(2,1)} %param.11), channel_id=1, source_target_pairs={{0,1},{1,0},{2,3},{3,2},{4,5},{5,4},{6,7},{7,6},{8,9},{9,8},{10,11... | collective-permute-start | bytes 1572872 | tf_op jit(solution)/shard_map/ppermute | solution.py:129
  1.9 1.1 %pad_maximum_fusion.own_ref = bf16[2,128,1024]{2,1,0:T(8,128)(2,1)S(1)} fusion(bf16[1,128,1024]{2,1,0:T(8,128)(2,1)} %bitcast.10, bf16[1,128,1024]{2,1,0:T(8,128)(2,1)} %bitcast.11), kind=kLoop, calls=%fused_computation.7 | loop fusion | flops 262144 | bytes 1048576 | tf_op jit(solution)/shard_map/stack | solution.py:138
  3.0 0.0 copy-start.1
  3.0 1.0 %collective-permute-start.3 = (bf16[2,128,1024]{2,1,0:T(8,128)(2,1)S(1)}, bf16[2,128,1024]{2,1,0:T(8,128)(2,1)S(1)}, u32[]{:S(2)}, u32[]{:S(2)}) collective-permute-start(bf16[2,128,1024]{2,1,0:T(8,128)(2,1)S(1)} %pad_maximum_fusion.own_ref), channel_id=1, source_target_pairs={{0,2},{2,0},{4,6},{6,4},{8,10},{10,8},{12,14},{14,12},{16,18},{18,... | collective-permute-start | bytes 1572872 | tf_op jit(solution)/shard_map/ppermute | solution.py:122
  4.0 3.0 %collective-permute-start.2 = (bf16[2,128,1024]{2,1,0:T(8,128)(2,1)S(1)}, bf16[2,128,1024]{2,1,0:T(8,128)(2,1)S(1)}, u32[]{:S(2)}, u32[]{:S(2)}) collective-permute-start(bf16[2,128,1024]{2,1,0:T(8,128)(2,1)S(1)} %pad_maximum_fusion.own_ref), channel_id=1, source_target_pairs={{6,2},{0,4},{10,6},{4,8},{14,10},{8,12},{18,14},{12,16},{22,18},{1... | collective-permute-start | bytes 1572872 | tf_op jit(solution)/shard_map/ppermute | solution.py:122
  7.1 2.2 %collective-permute-start = (bf16[2,128,1024]{2,1,0:T(8,128)(2,1)S(1)}, bf16[2,128,1024]{2,1,0:T(8,128)(2,1)S(1)}, u32[]{:S(2)}, u32[]{:S(2)}) collective-permute-start(bf16[2,128,1024]{2,1,0:T(8,128)(2,1)S(1)} %pad_maximum_fusion.own_ref), channel_id=1, source_target_pairs={{2,6},{4,0},{6,10},{8,4},{10,14},{12,8},{14,18},{16,12},{18,22},{2... | collective-permute-start | bytes 1572872 | tf_op jit(solution)/shard_map/ppermute | solution.py:122
  9.3 4.4 %collective-permute-done.1 = bf16[128,2048]{1,0:T(8,128)(2,1)S(1)} collective-permute-done((bf16[128,2048]{1,0:T(8,128)(2,1)}, bf16[128,2048]{1,0:T(8,128)(2,1)S(1)}, u32[]{:S(2)}, u32[]{:S(2)}) %collective-permute-start.1) | collective-permute-done | bytes 524320 | tf_op jit(solution)/shard_map/ppermute | solution.py:129
  13.7 1.1 %broadcast_select_fusion.1 = (bf16[128,2048]{1,0:T(8,128)(2,1)S(1)}, bf16[128,2048]{1,0:T(8,128)(2,1)S(1)}) fusion(bf16[128,2048]{1,0:T(8,128)(2,1)} %param.11, bf16[128,2048]{1,0:T(8,128)(2,1)S(1)} %collective-permute-done.1, pred[]{:T(512)S(6)} %eq.3), kind=kLoop, calls=%fused_computation.11 | loop fusion | flops 524288 | bytes 2097153 | tf_op jit(solution)/shard_map/jit(_where)/select_n | solution.py:132
  14.8 7.0 %convolution_convert_fusion.go_ref = bf16[128,1024]{1,0:T(8,128)(2,1)} fusion(bf16[1024,4096]{1,0:T(8,128)(2,1)} %param.10, bf16[128,2048]{1,0:T(8,128)(2,1)S(1)} %get-tuple-element.29, bf16[128,2048]{1,0:T(8,128)(2,1)S(1)} %get-tuple-element.28), kind=kOutput, calls=%fused_computation | convolution fusion | flops 1075970048 | bytes 9699328 | tf_op jit(solution)/shard_map/dot_general | solution.py:140
  21.8 8.8 %collective-permute-done.a_ref = bf16[2,128,1024]{2,1,0:T(8,128)(2,1)S(1)} collective-permute-done((bf16[2,128,1024]{2,1,0:T(8,128)(2,1)S(1)}, bf16[2,128,1024]{2,1,0:T(8,128)(2,1)S(1)}, u32[]{:S(2)}, u32[]{:S(2)}) %collective-permute-start) | collective-permute-done | bytes 524320 | tf_op jit(solution)/shard_map/ppermute | solution.py:122
  30.6 0.0 copy-start.4
  30.6 0.9 %collective-permute-start.4 = (bf16[2,128,1024]{2,1,0:T(8,128)(2,1)S(1)}, bf16[2,128,1024]{2,1,0:T(8,128)(2,1)S(1)}, u32[]{:S(2)}, u32[]{:S(2)}) collective-permute-start(bf16[2,128,1024]{2,1,0:T(8,128)(2,1)S(1)} %collective-permute-done.a_ref), channel_id=1, source_target_pairs={{0,2},{2,0},{4,6},{6,4},{8,10},{10,8},{12,14},{14,12},{16,18},{18,... | collective-permute-start | bytes 1572872 | tf_op jit(solution)/shard_map/ppermute | solution.py:122
  31.5 0.0 collective-permute-done.3.po_ref
  31.5 0.0 copy-start.2
  31.5 0.0 collective-permute-done.2.b_ref
  31.5 0.0 copy-start.3
  31.5 1.5 %collective-permute-done.4.pa_ref = bf16[2,128,1024]{2,1,0:T(8,128)(2,1)S(1)} collective-permute-done((bf16[2,128,1024]{2,1,0:T(8,128)(2,1)S(1)}, bf16[2,128,1024]{2,1,0:T(8,128)(2,1)S(1)}, u32[]{:S(2)}, u32[]{:S(2)}) %collective-permute-start.4) | collective-permute-done | bytes 524320 | tf_op jit(solution)/shard_map/ppermute | solution.py:122
  33.0 0.0 copy-start.7
  33.0 0.0 copy-done.1
  33.0 0.0 copy-done.4
  33.0 0.0 copy-done.2
  33.0 0.0 copy-done.3
  33.0 0.8 copy-done.7
  33.8 10.0 %shard_map.102 = (bf16[128,1024]{1,0:T(8,128)(2,1)}, bf16[128,1024]{1,0:T(8,128)(2,1)}, bf16[2,128,1024]{2,1,0:T(8,128)(2,1)}, bf16[2,128,1024]{2,1,0:T(8,128)(2...) custom-call(s32[1]{0:T(128)} %bitcast.index_ref, s32[16]{0:T(128)} %length_ref.1, ...), custom_call_target="tpu_custom_call" | custom-call | flops 8053063680 | bytes 6291456 | tf_op jit(solution)/shard_map/pallas_call | solution.py:88
  43.9 0.4 collective-permute-start.5
  44.3 1.7 %collective-permute-done.5 = bf16[2,128,1024]{2,1,0:T(8,128)(2,1)S(1)} collective-permute-done((bf16[2,128,1024]{2,1,0:T(8,128)(2,1)}, bf16[2,128,1024]{2,1,0:T(8,128)(2,1)S(1)}, u32[]{:S(2)}, u32[]{:S(2)}) %collective-permute-start.5) | collective-permute-done | bytes 524320 | tf_op jit(solution)/shard_map/ppermute | solution.py:122
  46.1 1.2 %add_convert_fusion.1 = bf16[2,128,1024]{2,1,0:T(8,128)(2,1)S(1)} fusion(bf16[2,128,1024]{2,1,0:T(8,128)(2,1)S(1)} %collective-permute-done.5, bf16[2,128,1024]{2,1,0:T(8,128)(2,1)} %get-tuple-element.17), kind=kLoop, calls=%fused_computation.6 | loop fusion | flops 1048576 | bytes 1572864 | tf_op jit(solution)/shard_map/convert_element_type | solution.py:156
  47.3 0.0 copy-start.6
  47.3 0.0 copy-start.5
  47.3 0.0 copy-start
  47.3 4.8 %fusion.6 = f32[128,4096]{1,0:T(8,128)S(1)} fusion(bf16[128,1024]{1,0:T(8,128)(2,1)} %get-tuple-element.20, bf16[1024,4096]{1,0:T(8,128)(2,1)} %param.10), kind=kOutput, calls=%fused_computation.15 | convolution fusion | flops 1073741824 | bytes 10747904 | tf_op jit(solution)/shard_map/dot_general | solution.py:166
  52.2 0.1 select_convert_fusion
  52.3 0.3 collective-permute-start.6
  52.6 0.0 copy-done.6
  52.6 0.7 collective-permute-start.7
  53.3 0.0 copy-done.5
  53.3 3.1 %collective-permute-start.8 = (bf16[2,128,1024]{2,1,0:T(8,128)(2,1)S(1)}, bf16[2,128,1024]{2,1,0:T(8,128)(2,1)S(1)}, u32[]{:S(2)}, u32[]{:S(2)}) collective-permute-start(bf16[2,128,1024]{2,1,0:T(8,128)(2,1)S(1)} %copy-done.5), channel_id=1, source_target_pairs={{2,6},{4,0},{6,10},{8,4},{10,14},{12,8},{14,18},{16,12},{18,22},{2... | collective-permute-start | bytes 1572872 | tf_op jit(solution)/shard_map/ppermute | solution.py:122
  56.4 3.1 %collective-permute-start.9 = (bf16[2,128,1024]{2,1,0:T(8,128)(2,1)S(1)}, bf16[2,128,1024]{2,1,0:T(8,128)(2,1)S(1)}, u32[]{:S(2)}, u32[]{:S(2)}) collective-permute-start(bf16[2,128,1024]{2,1,0:T(8,128)(2,1)S(1)} %add_convert_fusion.1), channel_id=1, source_target_pairs={{6,2},{0,4},{10,6},{4,8},{14,10},{8,12},{18,14},{12,16},{22,18},{1... | collective-permute-start | bytes 1572872 | tf_op jit(solution)/shard_map/ppermute | solution.py:122
  59.5 6.0 %collective-permute-done.6 = bf16[128,2048]{1,0:T(8,128)(2,1)S(1)} collective-permute-done((bf16[128,2048]{1,0:T(8,128)(2,1)S(1)}, bf16[128,2048]{1,0:T(8,128)(2,1)S(1)}, u32[]{:S(2)}, u32[]{:S(2)}) %collective-permute-start.6) | collective-permute-done | bytes 524320 | tf_op jit(solution)/shard_map/ppermute | solution.py:170
  65.5 1.0 %add_convert_fusion = bf16[128,2048]{1,0:T(8,128)(2,1)} fusion(bf16[128,2048]{1,0:T(8,128)(2,1)S(1)} %collective-permute-done.6, f32[128,4096]{1,0:T(8,128)S(1)} %fusion.6, pred[]{:T(512)S(6)} %eq.3), kind=kLoop, calls=%fused_computation.4 | loop fusion | flops 1048576 | bytes 3145729 | tf_op jit(solution)/shard_map/convert_element_type | solution.py:171
  66.5 0.0 collective-permute-done.7
  66.5 11.3 %collective-permute-done.8 = bf16[2,128,1024]{2,1,0:T(8,128)(2,1)S(1)} collective-permute-done((bf16[2,128,1024]{2,1,0:T(8,128)(2,1)S(1)}, bf16[2,128,1024]{2,1,0:T(8,128)(2,1)S(1)}, u32[]{:S(2)}, u32[]{:S(2)}) %collective-permute-start.8) | collective-permute-done | bytes 524320 | tf_op jit(solution)/shard_map/ppermute | solution.py:122
  77.8 2.8 %collective-permute-done.9 = bf16[2,128,1024]{2,1,0:T(8,128)(2,1)S(1)} collective-permute-done((bf16[2,128,1024]{2,1,0:T(8,128)(2,1)S(1)}, bf16[2,128,1024]{2,1,0:T(8,128)(2,1)S(1)}, u32[]{:S(2)}, u32[]{:S(2)}) %collective-permute-start.9) | collective-permute-done | bytes 524320 | tf_op jit(solution)/shard_map/ppermute | solution.py:122
  80.5 0.0 copy-done
  80.5 1.1 %fusion.4 = (bf16[128,1024]{1,0:T(8,128)(2,1)}, bf16[128,1024]{1,0:T(8,128)(2,1)}) fusion(bf16[2,128,1024]{2,1,0:T(8,128)(2,1)S(1)} %collective-permute-done.9, bf16[2,128,1024]{2,1,0:T(8,128)(2,1)S(1)} %collective-permute-done.8, bf16[2,128,1024]{2,1,0:T(8,128)(2,1)S(1)} %collective-permute-done.7, bf16[2,128,1024]{2,1,0:T(8,128)(2,1)S(1)} %copy-done), kind=kLoop, calls=%fused_computation.13 | loop fusion | flops 2097152 | bytes 2621440 | tf_op jit(solution)/shard_map/add | solution.py:161
Async XLA Ops:
  0.6 13.1 %collective-permute-start.1 = (bf16[128,2048]{1,0:T(8,128)(2,1)}, bf16[128,2048]{1,0:T(8,128)(2,1)S(1)}, u32[]{:S(2)}, u32[]{:S(2)}) collective-permute-start(bf16[128,2048]{1,0:T(8,128)(2,1)} %param.11), channel_id=1, source_target_pairs={{0,1},{1,0},{2,3},{3,2},{4,5},{5,4},{6,7},{7,6},{8,9},{9,8},{10,11... | collective-permute-start | bytes 1572872 | tf_op jit(solution)/shard_map/ppermute | solution.py:129
  3.0 30.0 %copy-start.1 = (bf16[2,128,1024]{2,1,0:T(8,128)(2,1)}, bf16[2,128,1024]{2,1,0:T(8,128)(2,1)S(1)}, u32[]{:S(2)}) copy-start(bf16[2,128,1024]{2,1,0:T(8,128)(2,1)S(1)} %pad_maximum_fusion.own_ref) | copy-start | bytes 1572868
  3.0 28.5 %collective-permute-start.3 = (bf16[2,128,1024]{2,1,0:T(8,128)(2,1)S(1)}, bf16[2,128,1024]{2,1,0:T(8,128)(2,1)S(1)}, u32[]{:S(2)}, u32[]{:S(2)}) collective-permute-start(bf16[2,128,1024]{2,1,0:T(8,128)(2,1)S(1)} %pad_maximum_fusion.own_ref), channel_id=1, source_target_pairs={{0,2},{2,0},{4,6},{6,4},{8,10},{10,8},{12,14},{14,12},{16,18},{18,... | collective-permute-start | bytes 1572872 | tf_op jit(solution)/shard_map/ppermute | solution.py:122
  4.0 27.5 %collective-permute-start.2 = (bf16[2,128,1024]{2,1,0:T(8,128)(2,1)S(1)}, bf16[2,128,1024]{2,1,0:T(8,128)(2,1)S(1)}, u32[]{:S(2)}, u32[]{:S(2)}) collective-permute-start(bf16[2,128,1024]{2,1,0:T(8,128)(2,1)S(1)} %pad_maximum_fusion.own_ref), channel_id=1, source_target_pairs={{6,2},{0,4},{10,6},{4,8},{14,10},{8,12},{18,14},{12,16},{22,18},{1... | collective-permute-start | bytes 1572872 | tf_op jit(solution)/shard_map/ppermute | solution.py:122
  7.1 23.6 %collective-permute-start = (bf16[2,128,1024]{2,1,0:T(8,128)(2,1)S(1)}, bf16[2,128,1024]{2,1,0:T(8,128)(2,1)S(1)}, u32[]{:S(2)}, u32[]{:S(2)}) collective-permute-start(bf16[2,128,1024]{2,1,0:T(8,128)(2,1)S(1)} %pad_maximum_fusion.own_ref), channel_id=1, source_target_pairs={{2,6},{4,0},{6,10},{8,4},{10,14},{12,8},{14,18},{16,12},{18,22},{2... | collective-permute-start | bytes 1572872 | tf_op jit(solution)/shard_map/ppermute | solution.py:122
  30.6 2.4 %copy-start.4 = (bf16[2,128,1024]{2,1,0:T(8,128)(2,1)}, bf16[2,128,1024]{2,1,0:T(8,128)(2,1)S(1)}, u32[]{:S(2)}) copy-start(bf16[2,128,1024]{2,1,0:T(8,128)(2,1)S(1)} %collective-permute-done.a_ref) | copy-start | bytes 1572868
  30.6 2.4 %collective-permute-start.4 = (bf16[2,128,1024]{2,1,0:T(8,128)(2,1)S(1)}, bf16[2,128,1024]{2,1,0:T(8,128)(2,1)S(1)}, u32[]{:S(2)}, u32[]{:S(2)}) collective-permute-start(bf16[2,128,1024]{2,1,0:T(8,128)(2,1)S(1)} %collective-permute-done.a_ref), channel_id=1, source_target_pairs={{0,2},{2,0},{4,6},{6,4},{8,10},{10,8},{12,14},{14,12},{16,18},{18,... | collective-permute-start | bytes 1572872 | tf_op jit(solution)/shard_map/ppermute | solution.py:122
  31.5 1.5 %copy-start.2 = (bf16[2,128,1024]{2,1,0:T(8,128)(2,1)}, bf16[2,128,1024]{2,1,0:T(8,128)(2,1)S(1)}, u32[]{:S(2)}) copy-start(bf16[2,128,1024]{2,1,0:T(8,128)(2,1)S(1)} %collective-permute-done.3.po_ref) | copy-start | bytes 1572868
  31.5 1.5 %copy-start.3 = (bf16[2,128,1024]{2,1,0:T(8,128)(2,1)}, bf16[2,128,1024]{2,1,0:T(8,128)(2,1)S(1)}, u32[]{:S(2)}) copy-start(bf16[2,128,1024]{2,1,0:T(8,128)(2,1)S(1)} %collective-permute-done.2.b_ref) | copy-start | bytes 1572868
  33.0 0.8 %copy-start.7 = (bf16[2,128,1024]{2,1,0:T(8,128)(2,1)}, bf16[2,128,1024]{2,1,0:T(8,128)(2,1)S(1)}, u32[]{:S(2)}) copy-start(bf16[2,128,1024]{2,1,0:T(8,128)(2,1)S(1)} %collective-permute-done.4.pa_ref) | copy-start | bytes 1572868
  43.9 2.2 %collective-permute-start.5 = (bf16[2,128,1024]{2,1,0:T(8,128)(2,1)}, bf16[2,128,1024]{2,1,0:T(8,128)(2,1)S(1)}, u32[]{:S(2)}, u32[]{:S(2)}) collective-permute-start(bf16[2,128,1024]{2,1,0:T(8,128)(2,1)} %get-tuple-element.18), channel_id=1, source_target_pairs={{0,2},{2,0},{4,6},{6,4},{8,10},{10,8},{12,14},{14,12},{16,18},{18,... | collective-permute-start | bytes 1572872 | tf_op jit(solution)/shard_map/ppermute | solution.py:122
  47.3 5.3 %copy-start.6 = (bf16[2,128,1024]{2,1,0:T(8,128)(2,1)S(1)}, bf16[2,128,1024]{2,1,0:T(8,128)(2,1)}, u32[]{:S(2)}) copy-start(bf16[2,128,1024]{2,1,0:T(8,128)(2,1)} %get-tuple-element.23) | copy-start | bytes 1572868
  47.3 5.9 %copy-start.5 = (bf16[2,128,1024]{2,1,0:T(8,128)(2,1)S(1)}, bf16[2,128,1024]{2,1,0:T(8,128)(2,1)}, u32[]{:S(2)}) copy-start(bf16[2,128,1024]{2,1,0:T(8,128)(2,1)} %get-tuple-element.24) | copy-start | bytes 1572868
  47.3 33.2 %copy-start = (bf16[2,128,1024]{2,1,0:T(8,128)(2,1)S(1)}, bf16[2,128,1024]{2,1,0:T(8,128)(2,1)}, u32[]{:S(2)}) copy-start(bf16[2,128,1024]{2,1,0:T(8,128)(2,1)} %get-tuple-element.22) | copy-start | bytes 1572868
  52.3 13.2 %collective-permute-start.6 = (bf16[128,2048]{1,0:T(8,128)(2,1)S(1)}, bf16[128,2048]{1,0:T(8,128)(2,1)S(1)}, u32[]{:S(2)}, u32[]{:S(2)}) collective-permute-start(bf16[128,2048]{1,0:T(8,128)(2,1)S(1)} %select_convert_fusion), channel_id=1, source_target_pairs={{0,1},{1,0},{2,3},{3,2},{4,5},{5,4},{6,7},{7,6},{8,9},{9,8},{10,11... | collective-permute-start | bytes 1572872 | tf_op jit(solution)/shard_map/ppermute | solution.py:170
  52.6 13.9 %collective-permute-start.7 = (bf16[2,128,1024]{2,1,0:T(8,128)(2,1)S(1)}, bf16[2,128,1024]{2,1,0:T(8,128)(2,1)S(1)}, u32[]{:S(2)}, u32[]{:S(2)}) collective-permute-start(bf16[2,128,1024]{2,1,0:T(8,128)(2,1)S(1)} %copy-done.6), channel_id=1, source_target_pairs={{0,2},{2,0},{4,6},{6,4},{8,10},{10,8},{12,14},{14,12},{16,18},{18,... | collective-permute-start | bytes 1572872 | tf_op jit(solution)/shard_map/ppermute | solution.py:122
  53.3 24.5 %collective-permute-start.8 = (bf16[2,128,1024]{2,1,0:T(8,128)(2,1)S(1)}, bf16[2,128,1024]{2,1,0:T(8,128)(2,1)S(1)}, u32[]{:S(2)}, u32[]{:S(2)}) collective-permute-start(bf16[2,128,1024]{2,1,0:T(8,128)(2,1)S(1)} %copy-done.5), channel_id=1, source_target_pairs={{2,6},{4,0},{6,10},{8,4},{10,14},{12,8},{14,18},{16,12},{18,22},{2... | collective-permute-start | bytes 1572872 | tf_op jit(solution)/shard_map/ppermute | solution.py:122
  56.4 24.2 %collective-permute-start.9 = (bf16[2,128,1024]{2,1,0:T(8,128)(2,1)S(1)}, bf16[2,128,1024]{2,1,0:T(8,128)(2,1)S(1)}, u32[]{:S(2)}, u32[]{:S(2)}) collective-permute-start(bf16[2,128,1024]{2,1,0:T(8,128)(2,1)S(1)} %add_convert_fusion.1), channel_id=1, source_target_pairs={{6,2},{0,4},{10,6},{4,8},{14,10},{8,12},{18,14},{12,16},{22,18},{1... | collective-permute-start | bytes 1572872 | tf_op jit(solution)/shard_map/ppermute | solution.py:122
